TPU v7x, 32 devices: a whole 2x2x4 slice. The times are simulated.
32 devices in a mesh: north: 8 (over y, x, core), deep: 4 (over z).
Axes of the slice: x: 2, y: 2, z: 4, core: 2. Of those that a mesh axis runs over, the one named last changes fastest.
Arguments:
- velocity: float32 [4, 128, 64, 256], P(None, None, 'north', 'deep'), may hold values from -6 to 6
- coupling: float32 [4, 4], replicated, may hold values from -4 to 4
- symbol_x: float32 [128], replicated, may hold values from 0.3 to 3
- symbol_y: float32 [64], replicated, may hold values from 0.3 to 3
- symbol_z: float32 [256], replicated, may hold values from 0.3 to 3
Outputs:
- spectrum: float32 [4, 128, 64, 256], P(None, 'north', 'deep')
All inputs are finite; a program needn't handle non-finite values.
Results may differ from a plain program's by a relative error of at most 0.00007.
Values sent between devices are 32-bit elements; how exact they have to be, the bound alone decides.
No kernel may reach another device: no remote copies, remote signals or barrier semaphores. Data moves between devices by JAX's collectives and lax.ppermute only.
A program may use at most 128 MiB of HBM per device.

v0:
```python
import jax
import jax.numpy as jnp
from jax import lax
from jax.sharding import PartitionSpec as P


def basis_table(count):
    rank = jnp.arange(count)
    angle = (
        jnp.pi
        / (count + 1)
        * ((rank[:, None] + 1) * (rank[None, :] + 1) % (2 * count + 2)).astype(jnp.float32)
    )
    return jnp.sin(angle) * (2.0 / (count + 1)) ** 0.5


def along_dim(values, dim):
    moved = jnp.tensordot(
        values, basis_table(values.shape[dim]), axes=([dim], [0]), precision=lax.Precision.HIGHEST
    )
    return jnp.moveaxis(moved, -1, dim)


def on_device(velocity, coupling, symbol_x, symbol_y, symbol_z):
    part_values = velocity
    part_values = along_dim(part_values, 1)
    part_values = lax.all_to_all(part_values, "north", split_axis=1, concat_axis=2, tiled=True)
    part_values = along_dim(part_values, 2)
    block_values = part_values
    block_values = lax.all_to_all(block_values, "deep", split_axis=2, concat_axis=3, tiled=True)
    block_values = along_dim(block_values, 3)
    share_x = block_values.shape[1]
    part_x = lax.dynamic_slice_in_dim(symbol_x, lax.axis_index("north") * share_x, share_x)
    share_y = block_values.shape[2]
    part_y = lax.dynamic_slice_in_dim(symbol_y, lax.axis_index("deep") * share_y, share_y)
    symbol = part_x[:, None, None] + part_y[None, :, None] + symbol_z[None, None, :]
    weight_xyz = 1.0 / (1.0 + symbol)
    mixed_fields = jnp.einsum(
        "ab,bxyz->axyz", coupling, block_values, precision=lax.Precision.HIGHEST
    )
    block_values = weight_xyz * block_values + (1.0 - weight_xyz) * mixed_fields
    return block_values


def solution(mesh):
    placed = (P(None, None, "north", "deep"), P(), P(), P(), P())
    return jax.shard_map(
        on_device,
        mesh=mesh,
        in_specs=placed,
        out_specs=P(None, "north", "deep", None),
        check_vma=False,
    )
```

profile of v0, /device:TPU:0, one launch (start us, length us, event | category | flops | bytes accessed | tf_op | source)
XLA Modules:
  0.0 92.6 jit_solution(7834806281157115720)
XLA Ops:
  0.0 1.2 %copy-done = f32[4,128,8,64]{1,3,2,0:T(8,128)S(1)} copy-done((f32[4,128,8,64]{1,3,2,0:T(8,128)S(1)}, f32[4,128,8,64]{1,3,2,0:T(8,128)}, u32[]{:S(2)}) %copy-start) | copy-done | bytes 1048600
  1.2 2.3 %fusion.29 = f32[128,2048]{0,1} fusion(f32[128,2048]{0,1:T(8,128)S(1)} %bitcast.42, s32[128]{0:T(128)S(1)} %iota_add_fusion.2), kind=kOutput, calls=%fused_computation.32 | convolution fusion | flops 402817024 | bytes 2097664
  3.5 3.1 %copy.17 = f32[4,128,8,64]{3,2,0,1:T(8,128)S(1)} copy(f32[4,128,8,64]{1,3,2,0:T(8,128)} %bitcast.47) | data formatting | bytes 2097152 | tf_op jit(solution)/shard_map/transpose | solution.py:21
  6.6 2.1 %reshape.72 = f32[8,1,32768]{2,1,0:T(1,128)} reshape(f32[128,4,8,64]{3,2,1,0:T(8,128)S(1)} %bitcast.44) | data formatting | bytes 2097152
  8.7 5.2 %all-to-all-start = ((f32[8,1,32768]{2,1,0:T(1,128)}), f32[8,1,32768]{2,1,0:T(1,128)S(1)}, u32[]{:S(2)}, u32[]{:S(2)}) async-start(f32[8,1,32768]{2,1,0:T(1,128)} %reshape.72), calls=%async_computation | async-start | bytes 2097152 | tf_op jit(solution)/shard_map/all_to_all | solution.py:27
  13.9 15.4 %all-to-all-done = f32[8,1,32768]{2,1,0:T(1,128)S(1)} async-done(((f32[8,1,32768]{2,1,0:T(1,128)}), f32[8,1,32768]{2,1,0:T(1,128)S(1)}, u32[]{:S(2)}, u32[]{:S(2)}) %all-to-all-start) | async-done | bytes 1048608 | tf_op jit(solution)/shard_map/all_to_all | solution.py:27
  29.3 0.6 broadcast.101
  29.8 4.5 %reduce = f32[8,32768]{1,0:T(8,128)} reduce(f32[8,1,32768]{2,1,0:T(1,128)S(1)} %all-to-all-done, f32[]{:T(128)} %broadcast.101), dimensions={1}, to_apply=%all_to_all.26.reduce_sub_computation | reduce | bytes 2097156 | tf_op jit(solution)/shard_map/all_to_all | solution.py:27
  34.3 2.1 %reshape.73 = f32[128,4,8,64]{3,2,1,0:T(8,128)S(1)} reshape(f32[8,32768]{1,0:T(8,128)} %reduce) | data formatting | bytes 2097152
  36.4 4.8 %fusion.3 = f32[4,16,64,64]{2,3,1,0:T(8,128)} fusion(f32[4,16,8,8,64]{4,3,0,1,2:T(8,128)S(1)} %bitcast.43, s32[64]{0:T(128)S(1)} %iota_add_fusion.1), kind=kOutput, calls=%fused_computation.3 | convolution fusion | flops 201367552 | bytes 2097408 | tf_op jit(solution)/shard_map/dot_general | solution.py:18
  41.2 3.1 %copy.21 = f32[4,16,64,64]{3,1,0,2:T(8,128)S(1)} copy(f32[4,16,64,64]{2,3,1,0:T(8,128)} %fusion.3) | data formatting | bytes 2097152 | tf_op jit(solution)/shard_map/transpose | solution.py:21
  44.3 2.4 %reshape.74 = f32[4,1,65536]{2,1,0:T(1,128)} reshape(f32[64,4,16,64]{3,2,1,0:T(8,128)S(1)} %bitcast.45) | data formatting | bytes 2097152
  46.8 4.9 %all-to-all-start.1 = ((f32[4,1,65536]{2,1,0:T(1,128)}), f32[4,1,65536]{2,1,0:T(1,128)S(1)}, u32[]{:S(2)}, u32[]{:S(2)}) async-start(f32[4,1,65536]{2,1,0:T(1,128)} %reshape.74), calls=%async_computation.1 | async-start | bytes 2097152 | tf_op jit(solution)/shard_map/all_to_all | solution.py:30
  51.6 0.1 dynamic_slice.7
  51.7 0.1 dynamic_slice.6
  51.9 0.8 add_divide_fusion
  52.7 21.9 %all-to-all-done.1 = f32[4,1,65536]{2,1,0:T(1,128)S(1)} async-done(((f32[4,1,65536]{2,1,0:T(1,128)}), f32[4,1,65536]{2,1,0:T(1,128)S(1)}, u32[]{:S(2)}, u32[]{:S(2)}) %all-to-all-start.1) | async-done | bytes 1048608 | tf_op jit(solution)/shard_map/all_to_all | solution.py:30
  74.6 4.6 %reduce.1 = f32[4,65536]{1,0:T(4,128)} reduce(f32[4,1,65536]{2,1,0:T(1,128)S(1)} %all-to-all-done.1, f32[]{:T(128)} %broadcast.101), dimensions={1}, to_apply=%all_to_all.30.reduce_sub_computation | reduce | bytes 2097156 | tf_op jit(solution)/shard_map/all_to_all | solution.py:30
  79.2 2.2 %reshape.75 = f32[64,4,16,64]{3,2,1,0:T(8,128)S(1)} reshape(f32[4,65536]{1,0:T(4,128)} %reduce.1) | data formatting | bytes 2097152
  81.4 2.7 %copy.23 = f32[4,16,16,4,64]{4,3,2,1,0:T(4,128)} copy(f32[4,16,16,4,64]{4,1,0,2,3:T(8,128)S(1)} %bitcast.46) | data formatting | bytes 2097152 | tf_op jit(solution)/shard_map/all_to_all | solution.py:30
  84.1 2.5 %all_to_all.33 = f32[4,16,16,256]{3,2,1,0:T(8,128)S(1)} reshape(f32[4,16,16,4,64]{4,3,2,1,0:T(4,128)} %copy.23) | data formatting | bytes 2097152 | tf_op jit(solution)/shard_map/all_to_all | solution.py:30
  86.7 2.1 %fusion.13 = f32[4,16,16,256]{3,2,1,0:T(8,128)S(1)} fusion(f32[4,16,16,256]{3,2,1,0:T(8,128)S(1)} %all_to_all.33, s32[256]{0:T(256)S(1)} %iota_add_fusion), kind=kOutput, calls=%fused_computation.14 | convolution fusion | flops 805961728 | bytes 2098176 | tf_op jit(solution)/shard_map/dot_general | solution.py:18
  88.8 2.5 %fusion.6 = f32[16,16,256,4]{2,3,1,0:T(4,128)S(1)} fusion(f32[4,16,16,256]{3,2,1,0:T(8,128)S(1)} %fusion.13, f32[4,4]{1,0:T(4,128)S(1)} %copy-done.2), kind=kOutput, calls=%fused_computation.6 | convolution fusion | flops 12582912 | bytes 2097216 | tf_op jit(solution)/shard_map/ab,bxyz->axyz/dot_general | solution.py:38
  91.3 1.3 %bitcast_add_fusion = f32[4,16,16,256]{3,2,1,0:T(8,128)} fusion(f32[16,16,256,4]{2,3,1,0:T(4,128)S(1)} %fusion.6, f32[4,16,16,256]{3,2,1,0:T(8,128)S(1)} %fusion.13, f32[16,16,256]{2,1,0:T(8,128)S(1)} %copy-done.1, f32[16,16,256]{2,1,0:T(8,128)S(1)} %get-tuple-element.5), kind=kLoop, calls=%fused_computation.4 | loop fusion | flops 786432 | bytes 3670016 | tf_op jit(solution)/shard_map/add | solution.py:41
  (15 shorter events, 0.1 us)
Async XLA Ops:
  0.0 1.2 %copy-start = (f32[4,128,8,64]{1,3,2,0:T(8,128)S(1)}, f32[4,128,8,64]{1,3,2,0:T(8,128)}, u32[]{:S(2)}) copy-start(f32[4,128,8,64]{1,3,2,0:T(8,128)} %param.5) | copy-start | bytes 3145732
  8.7 20.6 %all-to-all-start = ((f32[8,1,32768]{2,1,0:T(1,128)}), f32[8,1,32768]{2,1,0:T(1,128)S(1)}, u32[]{:S(2)}, u32[]{:S(2)}) async-start(f32[8,1,32768]{2,1,0:T(1,128)} %reshape.72), calls=%async_computation | async-start | bytes 2097152 | tf_op jit(solution)/shard_map/all_to_all | solution.py:27
  44.3 7.3 %copy-start.4 = (f32[64]{0:T(128)S(1)}, f32[64]{0:T(128)}, u32[]{:S(2)}) copy-start(f32[64]{0:T(128)} %param.8) | copy-start | bytes 772
  44.3 7.4 %copy-start.5 = (f32[128]{0:T(128)S(1)}, f32[128]{0:T(128)}, u32[]{:S(2)}) copy-start(f32[128]{0:T(128)} %param.7) | copy-start | bytes 1540
  44.3 7.5 %copy-start.3 = (f32[256]{0:T(256)S(1)}, f32[256]{0:T(256)}, u32[]{:S(2)}) copy-start(f32[256]{0:T(256)} %param.9) | copy-start | bytes 3076
  46.8 27.8 %all-to-all-start.1 = ((f32[4,1,65536]{2,1,0:T(1,128)}), f32[4,1,65536]{2,1,0:T(1,128)S(1)}, u32[]{:S(2)}, u32[]{:S(2)}) async-start(f32[4,1,65536]{2,1,0:T(1,128)} %reshape.74), calls=%async_computation.1 | async-start | bytes 2097152 | tf_op jit(solution)/shard_map/all_to_all | solution.py:30
  84.1 4.6 %copy-start.2 = (f32[4,4]{1,0:T(4,128)S(1)}, f32[4,4]{1,0:T(4,128)}, u32[]{:S(2)}) copy-start(f32[4,4]{1,0:T(4,128)} %param.6) | copy-start | bytes 196
  86.6 4.6 %copy-start.1 = (f32[16,16,256]{2,1,0:T(8,128)S(1)}, f32[16,16,256]{2,1,0:T(8,128)}, u32[]{:S(2)}) copy-start(f32[16,16,256]{2,1,0:T(8,128)} %get-tuple-element.6) | copy-start | bytes 786436
where the time goes:
time: 93.5 us; the launch traced here: 92.6 us
  waiting for transfers between devices  37.3 us (40%)
  local copies, waits for them, and re-layouts  22.1 us (24%)
  matrix products  11.6 us (12%)
  other arithmetic  11.3 us (12%)
  starting transfers between devices  10.1 us (11%)
    all_to_all x1, waiting for transfers between devices, on_device(): lax.all_to_all(block_values, 'deep', split_axis=2, concat_axis=3, tiled=T...  21.9 us
    all_to_all x1, waiting for transfers between devices, on_device(): lax.all_to_all(part_values, 'north', split_axis=1, concat_axis=2, tiled=T...  15.4 us
    unnamed x16, local copies, waits for them, and re-layouts  10.1 us
    dot_general x2, matrix products, along_dim(): jnp.tensordot(values, basis_table(values.shape[dim]), axes=([dim], [0]),...  6.89 us
    transpose x2, local copies, waits for them, and re-layouts, along_dim(): return jnp.moveaxis(moved, -1, dim)  6.15 us
    all_to_all x1, starting transfers between devices, on_device(): lax.all_to_all(part_values, 'north', split_axis=1, concat_axis=2, tiled=T...  5.2 us
    all_to_all x2, local copies, waits for them, and re-layouts, on_device(): lax.all_to_all(block_values, 'deep', split_axis=2, concat_axis=3, tiled=T...  5.19 us
    all_to_all x1, starting transfers between devices, on_device(): lax.all_to_all(block_values, 'deep', split_axis=2, concat_axis=3, tiled=T...  4.87 us
  transfers between devices with their start and end apart: 2, of which 2 were waited for; matrix products, arithmetic and copies ran while one was open for 1% of the time, Pallas kernels for 0%

commit v1 on v0

v1 whole, which is shorter than its diff:
```python
import functools

import jax
import jax.numpy as jnp
import numpy as np
from jax import lax
from jax.experimental import pallas as pl
from jax.experimental.pallas import tpu as pltpu
from jax.sharding import PartitionSpec as P

SHARES = (1.0,)


def basis_table(count):
    rank = np.arange(1, count + 1)
    turn = (rank[:, None] * rank[None, :]) % (2 * count + 2)
    return (np.sin(np.pi * turn / (count + 1)) * np.sqrt(2.0 / (count + 1))).astype(np.float32)


def halves(values):
    high = values.astype(jnp.bfloat16)
    low = (values - high.astype(jnp.float32)).astype(jnp.bfloat16)
    return high, low


def product(left, right, dims):
    dot = functools.partial(
        lax.dot_general, dimension_numbers=(dims, ((), ())), preferred_element_type=jnp.float32
    )
    left_high, left_low = left
    right_high, right_low = right
    return dot(left_high, right_high) + (dot(left_high, right_low) + dot(left_low, right_high))


def x_kernel(values_ref, high_ref, low_ref, out_ref):
    fields, lines, depth, count = values_ref.shape
    groups, pieces, rows, width = out_ref.shape
    share = rows // lines
    table = (high_ref[...], low_ref[...])
    for line in range(lines):
        plane = values_ref[:, line].reshape(fields * depth, count)
        modes = product(table, halves(plane), ((1,), (1,)))
        for group in range(groups):
            for piece in range(pieces):
                out_ref[group, piece, pl.ds(line, share, stride=lines), :] = modes[
                    group * share : (group + 1) * share, piece * width : (piece + 1) * width
                ]


def y_kernel(values_ref, high_ref, low_ref, out_ref):
    sources, pieces, rows, width = values_ref.shape
    groups, share, block, _ = out_ref.shape
    lines = rows // share
    table = (high_ref[...], low_ref[...])
    for mode in range(share):
        plane = jnp.concatenate(
            [
                values_ref[:, piece, mode * lines : (mode + 1) * lines, :].reshape(-1, width)
                for piece in range(pieces)
            ],
            axis=1,
        )
        modes = product(table, halves(plane), ((1,), (0,)))
        for group in range(groups):
            out_ref[group, mode] = modes[group * block : (group + 1) * block]


def z_values(values_ref, high_ref, low_ref, fields):
    sources, share, block, lanes = values_ref.shape
    depth = lanes // fields
    table = (high_ref[...], low_ref[...])
    planes = [values_ref[source].reshape(share * block, lanes) for source in range(sources)]
    spectra = []
    for field in range(fields):
        line = jnp.concatenate(
            [plane[:, field * depth : (field + 1) * depth] for plane in planes], axis=1
        )
        spectra.append(product(halves(line), table, ((1,), (0,))))
    return spectra


def z_kernel(first, *refs):
    values_ref, high_ref, low_ref, weight_ref, coupling_ref = refs[:5]
    out_ref, staged, sems = refs[-3:]
    fields = staged.shape[0]
    _, share, block, _ = values_ref.shape
    spectra = z_values(values_ref, high_ref, low_ref, fields)
    weight = weight_ref[...].reshape(share * block, -1)
    copies = []
    for field in range(fields):
        mixed = spectra[0] * coupling_ref[field, 0]
        for other in range(1, fields):
            mixed += spectra[other] * coupling_ref[field, other]
        new = mixed + weight * (spectra[field] - mixed)
        staged[field] = new.reshape(share, block, -1)
        copy = pltpu.make_async_copy(
            staged.at[field], out_ref.at[field, pl.ds(first, share)], sems.at[field]
        )
        copy.start()
        copies.append(copy)
    for copy in copies:
        copy.wait()


def split_table(table):
    table = np.asarray(table, np.float32)
    high = jnp.asarray(table).astype(jnp.bfloat16)
    low = (jnp.asarray(table) - high.astype(jnp.float32)).astype(jnp.bfloat16)
    return high, low


def np_split(table):
    high = table.astype(jnp.bfloat16)
    low = (table - high.astype(np.float32)).astype(jnp.bfloat16)
    return jnp.asarray(high), jnp.asarray(low)


VMEM = pl.BlockSpec(memory_space=pltpu.VMEM)


def cost(flops, moved):
    return pl.CostEstimate(flops=int(flops), bytes_accessed=int(moved), transcendentals=0)


def chunks_of(share):
    bounds, total = [0], 0.0
    for part in SHARES:
        total += part
        bounds.append(round(share * total / sum(SHARES)))
    return [(a, b - a) for a, b in zip(bounds, bounds[1:]) if b > a]


def on_device(north, deep, velocity, coupling, symbol_x, symbol_y, symbol_z):
    fields, count_x, lines, depth = velocity.shape
    count_y, count_z = lines * north, depth * deep
    share_x, share_y = count_x // north, count_y // deep
    lanes = fields * depth
    width = 128 if lanes % 128 == 0 else lanes
    table_x = basis_table(count_x).reshape(north, share_x, count_x)
    high_y, low_y = np_split(basis_table(count_y))
    high_z, low_z = np_split(basis_table(count_z))
    values = jnp.transpose(velocity, (0, 2, 3, 1))
    part_x = lax.dynamic_slice_in_dim(symbol_x, lax.axis_index("north") * share_x, share_x)
    part_y = lax.dynamic_slice_in_dim(symbol_y, lax.axis_index("deep") * share_y, share_y)
    weight = 1.0 / (1.0 + (part_x[:, None, None] + part_y[None, :, None] + symbol_z))
    out = None
    for first, share in chunks_of(share_x):
        high, low = np_split(table_x[:, first : first + share].reshape(north * share, count_x))
        sent = pl.pallas_call(
            x_kernel,
            out_shape=jax.ShapeDtypeStruct((north, lanes // width, share * lines, width), jnp.float32),
            in_specs=[VMEM] * 3,
            out_specs=VMEM,
            cost_estimate=cost(6 * north * share * count_x * lines * lanes, 4 * values.size),
            name="x_modes",
        )(values, high, low)
        lines_here = lax.all_to_all(sent, "north", split_axis=0, concat_axis=0, tiled=True)
        sent = pl.pallas_call(
            y_kernel,
            out_shape=jax.ShapeDtypeStruct((deep, share, share_y, lanes), jnp.float32),
            in_specs=[VMEM] * 3,
            out_specs=VMEM,
            cost_estimate=cost(6 * count_y * count_y * share * lanes, 8 * sent.size),
            name="y_modes",
        )(lines_here, high_y, low_y)
        lines_here = lax.all_to_all(sent, "deep", split_axis=0, concat_axis=0, tiled=True)
        operands = [lines_here, high_z, low_z, weight[first : first + share], coupling]
        specs = [VMEM] * 4 + [pl.BlockSpec(memory_space=pltpu.SMEM)]
        aliases = {}
        if out is not None:
            operands.append(out)
            specs.append(pl.BlockSpec(memory_space=pl.ANY))
            aliases = {5: 0}
        out = pl.pallas_call(
            functools.partial(z_kernel, first),
            out_shape=jax.ShapeDtypeStruct((fields, share_x, share_y, count_z), jnp.float32),
            in_specs=specs,
            out_specs=pl.BlockSpec(memory_space=pl.ANY),
            scratch_shapes=[
                pltpu.VMEM((fields, share, share_y, count_z), jnp.float32),
                pltpu.SemaphoreType.DMA((fields,)),
            ],
            input_output_aliases=aliases,
            cost_estimate=cost(6 * sent.size * count_z, 8 * sent.size),
            name="z_modes",
        )(*operands)
    return out


def solution(mesh):
    placed = (P(None, None, "north", "deep"), P(), P(), P(), P())
    return jax.shard_map(
        functools.partial(on_device, mesh.shape["north"], mesh.shape["deep"]),
        mesh=mesh,
        in_specs=placed,
        out_specs=P(None, "north", "deep", None),
        check_vma=False,
    )
```

time: 93.5 us -> 61.2 us (0.65)
  blocking collectives: 0 us -> 20.6 us
  local copies, waits for them, and re-layouts: 22.1 us -> 3.04 us
  waiting for transfers between devices: 37.3 us -> 22.2 us
  matrix products: 11.6 us -> 0 us
  other arithmetic: 11.3 us -> 0.87 us
  Pallas kernels: 0 us -> 8.84 us
  starting transfers between devices: 10.1 us -> 5.26 us
    all_to_all x0 -> x1, blocking collectives: none -> 20.6 us  [on_device(): lax.all_to_all(sent, 'north', split_axis=0, concat_axis=0, tiled=True)]
    all_to_all x2 -> x1, waiting for transfers between devices: 37.3 us -> 22.2 us  [on_device(): lax.all_to_all(sent, 'deep', split_axis=0, concat_axis=0, tiled=True)]
    dot_general x3 -> x0, matrix products: 9.38 us -> none  [the longest x2 6.89 us: along_dim(): jnp.tensordot(values, basis_table(values.shape[dim]), axes=([dim], [0]),...]
    all_to_all x2 -> x0, other arithmetic: 9.11 us -> none  [the longest x1 4.63 us: on_device(): lax.all_to_all(block_values, 'deep', split_axis=2, concat_axis=3, tiled=T...]
    pallas_call x0 -> x3, Pallas kernels: none -> 8.84 us  [the longest x1 3.26 us: on_device(): pl.pallas_call(functools.partial(z_kernel, first), out_shape=jax.ShapeDty...]
    unnamed x16 -> x8, local copies, waits for them, and re-layouts: 10.1 us -> 2.89 us
    transpose x2 -> x0, local copies, waits for them, and re-layouts: 6.15 us -> none  [along_dim(): return jnp.moveaxis(moved, -1, dim)]
    all_to_all x3 -> x0, local copies, waits for them, and re-layouts: 5.77 us -> none  [the longest x2 5.19 us: on_device(): lax.all_to_all(block_values, 'deep', split_axis=2, concat_axis=3, tiled=T...]
  transfers between devices with their start and end apart: 2 -> 1, of which waited for: 2 -> 1; matrix products, arithmetic and copies ran while one was open for 1% -> 2% of each run, Pallas kernels for 0% -> 0%
where the time goes in v1:
time: 61.2 us; the launch traced here: 60.9 us
  waiting for transfers between devices  22.2 us (36%)
  blocking collectives  20.6 us (34%)
  Pallas kernels  8.84 us (14%)
  starting transfers between devices  5.26 us (9%)
  local copies, waits for them, and re-layouts  3.04 us (5%)
  other arithmetic  0.87 us (1%)
    all_to_all x1, waiting for transfers between devices, on_device(): lax.all_to_all(sent, 'deep', split_axis=0, concat_axis=0, tiled=True)  22.2 us
    all_to_all x1, blocking collectives, on_device(): lax.all_to_all(sent, 'north', split_axis=0, concat_axis=0, tiled=True)  20.6 us
    all_to_all x1, starting transfers between devices, on_device(): lax.all_to_all(sent, 'deep', split_axis=0, concat_axis=0, tiled=True)  5.26 us
    pallas_call x1, Pallas kernels, on_device(): pl.pallas_call(functools.partial(z_kernel, first), out_shape=jax.ShapeDty...  3.26 us
    unnamed x8, local copies, waits for them, and re-layouts  2.89 us
    pallas_call x1, Pallas kernels, on_device(): pl.pallas_call(x_kernel, out_shape=jax.ShapeDtypeStruct((north, lanes //...  2.82 us
    pallas_call x1, Pallas kernels, on_device(): pl.pallas_call(y_kernel, out_shape=jax.ShapeDtypeStruct((deep, share, sha...  2.76 us
  transfers between devices with their start and end apart: 1, of which 1 were waited for; matrix products, arithmetic and copies ran while one was open for 2% of the time, Pallas kernels for 0%

profile of v1, /device:TPU:0, one launch (start us, length us, event | category | flops | bytes accessed | tf_op | source)
XLA Modules:
  0.0 60.9 jit_solution(15753255257551513691)
XLA Ops:
  0.0 2.8 %x_modes.1 = f32[8,2,128,128]{3,2,1,0:T(8,128)} custom-call(f32[4,8,64,128]{3,2,1,0:T(8,128)} %bitcast.1, bf16[128,128]{1,0:T(8,128)(2,1)} %constant.35.clone.high_ref, bf16[128,128]{1,0:T(8,128)(2,1)} %constant.36.clone.low_ref), custom_call_target="tpu_custom_call" | custom-call | flops 201326592 | bytes 1048576 | tf_op jit(solution)/shard_map/x_modes/pallas_call | solution.py:149
  2.8 20.6 %all_to_all.10.values_ref = f32[8,2,128,128]{3,2,1,0:T(8,128)} all-to-all(f32[8,2,128,128]{3,2,1,0:T(8,128)} %x_modes.1), channel_id=1, replica_groups=mesh['north'=8,'deep'=4] {'north'}, dimensions={0} | all-to-all | bytes 2097152 | tf_op jit(solution)/shard_map/all_to_all | solution.py:157
  23.5 2.8 %y_modes.1 = f32[4,16,16,256]{3,2,1,0:T(8,128)} custom-call(f32[8,2,128,128]{3,2,1,0:T(8,128)} %all_to_all.10.values_ref, bf16[64,64]{1,0:T(8,128)(2,1)} %constant.31.clone.high_ref, bf16[64,64]{1,0:T(8,128)(2,1)} %constant.32.clone.low_ref), custom_call_target="tpu_custom_call" | custom-call | flops 100663296 | bytes 2097152 | tf_op jit(solution)/shard_map/y_modes/pallas_call | solution.py:158
  26.2 5.3 %all-to-all-start.1 = ((f32[4,16,16,256]{3,2,1,0:T(8,128)}), f32[4,16,16,256]{3,2,1,0:T(8,128)S(1)}, u32[]{:S(2)}, u32[]{:S(2)}) async-start(f32[4,16,16,256]{3,2,1,0:T(8,128)} %y_modes.1), calls=%async_computation.1 | async-start | bytes 2097152 | tf_op jit(solution)/shard_map/all_to_all | solution.py:166
  31.5 0.0 copy-start.2
  31.5 0.7 %copy-done.2 = f32[64]{0:T(128)S(1)} copy-done((f32[64]{0:T(128)S(1)}, f32[64]{0:T(128)}, u32[]{:S(2)}) %copy-start.2) | copy-done | bytes 280
  32.1 0.1 dynamic_slice.7
  32.2 0.0 copy-start.3
  32.2 0.7 %copy-done.3 = f32[128]{0:T(128)S(1)} copy-done((f32[128]{0:T(128)S(1)}, f32[128]{0:T(128)}, u32[]{:S(2)}) %copy-start.3) | copy-done | bytes 536
  32.9 0.1 dynamic_slice.6
  32.9 0.0 copy-start.1
  32.9 0.1 broadcast_add_fusion
  33.0 0.6 copy-done.1
  33.6 0.8 %add_divide_fusion.refs_3_ = f32[16,16,256]{2,1,0:T(8,128)} fusion(f32[256]{0:T(256)S(1)} %copy-done.1, f32[16,16]{1,0:T(8,128)S(1)} %broadcast_add_fusion), kind=kLoop, calls=%fused_computation | loop fusion | flops 196608 | bytes 264192 | tf_op jit(solution)/shard_map/div | solution.py:145
  34.4 22.2 %all-to-all-done.1.refs_0_ = f32[4,16,16,256]{3,2,1,0:T(8,128)S(1)} async-done(((f32[4,16,16,256]{3,2,1,0:T(8,128)}), f32[4,16,16,256]{3,2,1,0:T(8,128)S(1)}, u32[]{:S(2)}, u32[]{:S(2)}) %all-to-all-start.1) | async-done | bytes 1048608 | tf_op jit(solution)/shard_map/all_to_all | solution.py:166
  56.7 0.0 copy-start
  56.7 1.0 %copy-done = f32[4,16,16,256]{3,2,1,0:T(8,128)} copy-done((f32[4,16,16,256]{3,2,1,0:T(8,128)}, f32[4,16,16,256]{3,2,1,0:T(8,128)S(1)}, u32[]{:S(2)}) %copy-start) | copy-done | bytes 1048600
  57.6 3.3 %z_modes.1 = f32[4,16,16,256]{3,2,1,0:T(8,128)} custom-call(f32[4,16,16,256]{3,2,1,0:T(8,128)} %copy-done, bf16[256,256]{1,0:T(8,128)(2,1)} %constant.33.clone.refs_1_, bf16[256,256]{1,0:T(8,128)(2,1)} %constant.34.clone.refs_2_, f32[16,16,256]{2,1,0:T(8,128)} %add_divide_fusion.refs_3_, f32[4,4]{1,0:T(4,128)} %refs_4_.1), custom_call_target="tpu_custom_call" | custom-call | flops 402653184 | bytes 2097152 | tf_op jit(solution)/shard_map/z_modes/pallas_call | solution.py:174
Async XLA Ops:
  26.2 30.4 %all-to-all-start.1 = ((f32[4,16,16,256]{3,2,1,0:T(8,128)}), f32[4,16,16,256]{3,2,1,0:T(8,128)S(1)}, u32[]{:S(2)}, u32[]{:S(2)}) async-start(f32[4,16,16,256]{3,2,1,0:T(8,128)} %y_modes.1), calls=%async_computation.1 | async-start | bytes 2097152 | tf_op jit(solution)/shard_map/all_to_all | solution.py:166
  31.5 0.7 %copy-start.2 = (f32[64]{0:T(128)S(1)}, f32[64]{0:T(128)}, u32[]{:S(2)}) copy-start(f32[64]{0:T(128)} %param.14) | copy-start | bytes 772
  32.2 0.7 %copy-start.3 = (f32[128]{0:T(128)S(1)}, f32[128]{0:T(128)}, u32[]{:S(2)}) copy-start(f32[128]{0:T(128)} %param.13) | copy-start | bytes 1540
  32.9 0.7 %copy-start.1 = (f32[256]{0:T(256)S(1)}, f32[256]{0:T(256)}, u32[]{:S(2)}) copy-start(f32[256]{0:T(256)} %param.15) | copy-start | bytes 3076
  56.7 1.0 %copy-start = (f32[4,16,16,256]{3,2,1,0:T(8,128)}, f32[4,16,16,256]{3,2,1,0:T(8,128)S(1)}, u32[]{:S(2)}) copy-start(f32[4,16,16,256]{3,2,1,0:T(8,128)S(1)} %all-to-all-done.1.refs_0_) | copy-start | bytes 3145732

commit v2 on v1

--- a/solution.py
+++ b/solution.py
@@ -151,6 +151,7 @@
             out_shape=jax.ShapeDtypeStruct((north, lanes // width, share * lines, width), jnp.float32),
             in_specs=[VMEM] * 3,
             out_specs=VMEM,
+            compiler_params=pltpu.CompilerParams(vmem_limit_bytes=16 * 2**20),
             cost_estimate=cost(6 * north * share * count_x * lines * lanes, 4 * values.size),
             name="x_modes",
         )(values, high, low)
@@ -160,6 +161,7 @@
             out_shape=jax.ShapeDtypeStruct((deep, share, share_y, lanes), jnp.float32),
             in_specs=[VMEM] * 3,
             out_specs=VMEM,
+            compiler_params=pltpu.CompilerParams(vmem_limit_bytes=16 * 2**20),
             cost_estimate=cost(6 * count_y * count_y * share * lanes, 8 * sent.size),
             name="y_modes",
         )(lines_here, high_y, low_y)
@@ -181,6 +183,7 @@
                 pltpu.SemaphoreType.DMA((fields,)),
             ],
             input_output_aliases=aliases,
+            compiler_params=pltpu.CompilerParams(vmem_limit_bytes=16 * 2**20),
             cost_estimate=cost(6 * sent.size * count_z, 8 * sent.size),
             name="z_modes",
         )(*operands)

time: 61.2 us -> 58.2 us (0.951)
  Pallas kernels: 8.84 us -> 4.58 us
  local copies, waits for them, and re-layouts: 3.04 us -> 4.83 us
  waiting for transfers between devices: 22.2 us -> 22.9 us
  other arithmetic: 0.87 us -> 0.18 us
    pallas_call x1, Pallas kernels: 2.82 us -> 0.61 us  [on_device(): pl.pallas_call(x_kernel, out_shape=jax.ShapeDtypeStruct((north, lanes //...]
    unnamed x8 -> x22, local copies, waits for them, and re-layouts: 2.89 us -> 4.68 us
    pallas_call x1, Pallas kernels: 2.76 us -> 1.52 us  [on_device(): pl.pallas_call(y_kernel, out_shape=jax.ShapeDtypeStruct((deep, share, sha...]
    pallas_call x1, Pallas kernels: 3.26 us -> 2.44 us  [on_device(): pl.pallas_call(functools.partial(z_kernel, first), out_shape=jax.ShapeDty...]
    div x1, other arithmetic: 0.8 us -> 0.11 us  [on_device(): 1.0 / (1.0 + (part_x[:, None, None] + part_y[None, :, None] + symbol_z))]
    all_to_all x1, waiting for transfers between devices: 22.2 us -> 22.9 us  [on_device(): lax.all_to_all(sent, 'deep', split_axis=0, concat_axis=0, tiled=True)]
  transfers between devices with their start and end apart: 1 -> 1, of which waited for: 1 -> 1; matrix products, arithmetic and copies ran while one was open for 2% -> 1% of each run, Pallas kernels for 0% -> 0%
where the time goes in v2:
time: 58.2 us; the launch traced here: 57.7 us
  waiting for transfers between devices  22.9 us (39%)
  blocking collectives  20.3 us (35%)
  starting transfers between devices  4.87 us (8%)
  local copies, waits for them, and re-layouts  4.83 us (8%)
  Pallas kernels  4.58 us (8%)
    all_to_all x1, waiting for transfers between devices, on_device(): lax.all_to_all(sent, 'deep', split_axis=0, concat_axis=0, tiled=True)  22.9 us
    all_to_all x1, blocking collectives, on_device(): lax.all_to_all(sent, 'north', split_axis=0, concat_axis=0, tiled=True)  20.3 us
    all_to_all x1, starting transfers between devices, on_device(): lax.all_to_all(sent, 'deep', split_axis=0, concat_axis=0, tiled=True)  4.87 us
    unnamed x22, local copies, waits for them, and re-layouts  4.68 us
    pallas_call x1, Pallas kernels, on_device(): pl.pallas_call(functools.partial(z_kernel, first), out_shape=jax.ShapeDty...  2.44 us
    pallas_call x1, Pallas kernels, on_device(): pl.pallas_call(y_kernel, out_shape=jax.ShapeDtypeStruct((deep, share, sha...  1.52 us
  transfers between devices with their start and end apart: 1, of which 1 were waited for; matrix products, arithmetic and copies ran while one was open for 1% of the time, Pallas kernels for 0%

profile of v2, /device:TPU:0, one launch (start us, length us, event | category | flops | bytes accessed | tf_op | source)
XLA Modules:
  0.0 57.7 jit_solution(7262263535436254536)
XLA Ops:
  0.0 0.0 copy-start
  0.0 1.2 %copy-done = f32[4,128,8,64]{1,3,2,0:T(8,128)S(1)} copy-done((f32[4,128,8,64]{1,3,2,0:T(8,128)S(1)}, f32[4,128,8,64]{1,3,2,0:T(8,128)}, u32[]{:S(2)}) %copy-start) | copy-done | bytes 1048600
  1.2 0.8 %copy-done.3 = bf16[128,128]{1,0:T(8,128)(2,1)S(1)} copy-done((bf16[128,128]{1,0:T(8,128)(2,1)S(1)}, bf16[128,128]{1,0:T(8,128)(2,1)}, u32[]{:S(2)}) %copy-start.3) | copy-done | bytes 32792
  2.0 0.8 %copy-done.4 = bf16[128,128]{1,0:T(8,128)(2,1)S(1)} copy-done((bf16[128,128]{1,0:T(8,128)(2,1)S(1)}, bf16[128,128]{1,0:T(8,128)(2,1)}, u32[]{:S(2)}) %copy-start.4) | copy-done | bytes 32792
  2.7 0.6 %x_modes.1 = f32[8,2,128,128]{3,2,1,0:T(8,128)S(1)} custom-call(f32[4,8,64,128]{3,2,1,0:T(8,128)S(1)} %bitcast.1, bf16[128,128]{1,0:T(8,128)(2,1)S(1)} %copy-done.3, bf16[128,128]{1,0:T(8,128)(2,1)S(1)} %copy-done.4), custom_call_target="tpu_custom_call" | custom-call | flops 201326592 | bytes 1048576 | tf_op jit(solution)/shard_map/x_modes/pallas_call | solution.py:149
  3.4 0.0 copy-start.5
  3.4 0.0 copy-start.6
  3.4 20.3 %all_to_all.10.values_ref = f32[8,2,128,128]{3,2,1,0:T(8,128)S(1)} all-to-all(f32[8,2,128,128]{3,2,1,0:T(8,128)S(1)} %x_modes.1), channel_id=1, replica_groups=mesh['north'=8,'deep'=4] {'north'}, dimensions={0} | all-to-all | bytes 2097152 | tf_op jit(solution)/shard_map/all_to_all | solution.py:158
  23.7 0.0 copy-done.5
  23.7 0.0 copy-done.6
  23.7 1.5 %y_modes.1 = f32[4,16,16,256]{3,2,1,0:T(8,128)} custom-call(f32[8,2,128,128]{3,2,1,0:T(8,128)S(1)} %all_to_all.10.values_ref, bf16[64,64]{1,0:T(8,128)(2,1)S(1)} %copy-done.5, bf16[64,64]{1,0:T(8,128)(2,1)S(1)} %copy-done.6), custom_call_target="tpu_custom_call" | custom-call | flops 100663296 | bytes 2097152 | tf_op jit(solution)/shard_map/y_modes/pallas_call | solution.py:159
  25.2 4.9 %all-to-all-start.1 = ((f32[4,16,16,256]{3,2,1,0:T(8,128)}), f32[4,16,16,256]{3,2,1,0:T(8,128)S(1)}, u32[]{:S(2)}, u32[]{:S(2)}) async-start(f32[4,16,16,256]{3,2,1,0:T(8,128)} %y_modes.1), calls=%async_computation.1 | async-start | bytes 2097152 | tf_op jit(solution)/shard_map/all_to_all | solution.py:168
  30.1 0.7 %copy-done.9 = f32[64]{0:T(128)S(1)} copy-done((f32[64]{0:T(128)S(1)}, f32[64]{0:T(128)}, u32[]{:S(2)}) %copy-start.9) | copy-done | bytes 280
  30.8 0.1 dynamic_slice.7
  30.8 0.7 %copy-done.10 = f32[128]{0:T(128)S(1)} copy-done((f32[128]{0:T(128)S(1)}, f32[128]{0:T(128)}, u32[]{:S(2)}) %copy-start.10) | copy-done | bytes 536
  31.5 0.1 dynamic_slice.6
  31.6 0.1 broadcast_add_fusion
  31.6 0.6 %copy-done.8 = f32[256]{0:T(256)S(1)} copy-done((f32[256]{0:T(256)S(1)}, f32[256]{0:T(256)}, u32[]{:S(2)}) %copy-start.8) | copy-done | bytes 1048
  32.3 0.1 add_divide_fusion.refs_3_
  32.4 22.9 %all-to-all-done.1.refs_0_ = f32[4,16,16,256]{3,2,1,0:T(8,128)S(1)} async-done(((f32[4,16,16,256]{3,2,1,0:T(8,128)}), f32[4,16,16,256]{3,2,1,0:T(8,128)S(1)}, u32[]{:S(2)}, u32[]{:S(2)}) %all-to-all-start.1) | async-done | bytes 1048608 | tf_op jit(solution)/shard_map/all_to_all | solution.py:168
  55.3 0.0 copy-done.1
  55.3 0.0 copy-done.2
  55.3 0.0 copy-done.7
  55.3 2.4 %z_modes.1 = f32[4,16,16,256]{3,2,1,0:T(8,128)} custom-call(f32[4,16,16,256]{3,2,1,0:T(8,128)S(1)} %all-to-all-done.1.refs_0_, bf16[256,256]{1,0:T(8,128)(2,1)S(1)} %copy-done.1, bf16[256,256]{1,0:T(8,128)(2,1)S(1)} %copy-done.2, f32[16,16,256]{2,1,0:T(8,128)S(1)} %add_divide_fusion.refs_3_, f32[4,4]{1,0:T(4,128)S(1)} %copy-done.7), custom_call_target="tpu_custom_call" | custom-call | flops 402653184 | bytes 2097152 | tf_op jit(solution)/shard_map/z_modes/pallas_call | solution.py:176
  (8 shorter events, 0.0 us)
Async XLA Ops:
  0.0 1.2 %copy-start = (f32[4,128,8,64]{1,3,2,0:T(8,128)S(1)}, f32[4,128,8,64]{1,3,2,0:T(8,128)}, u32[]{:S(2)}) copy-start(f32[4,128,8,64]{1,3,2,0:T(8,128)} %param.11) | copy-start | bytes 3145732
  1.2 0.8 %copy-start.3 = (bf16[128,128]{1,0:T(8,128)(2,1)S(1)}, bf16[128,128]{1,0:T(8,128)(2,1)}, u32[]{:S(2)}) copy-start(bf16[128,128]{1,0:T(8,128)(2,1)} %constant.35.clone.high_ref) | copy-start | bytes 98308
  2.0 0.8 %copy-start.4 = (bf16[128,128]{1,0:T(8,128)(2,1)S(1)}, bf16[128,128]{1,0:T(8,128)(2,1)}, u32[]{:S(2)}) copy-start(bf16[128,128]{1,0:T(8,128)(2,1)} %constant.36.clone.low_ref) | copy-start | bytes 98308
  3.4 20.4 %copy-start.5 = (bf16[64,64]{1,0:T(8,128)(2,1)S(1)}, bf16[64,64]{1,0:T(8,128)(2,1)}, u32[]{:S(2)}) copy-start(bf16[64,64]{1,0:T(8,128)(2,1)} %constant.31.clone.high_ref) | copy-start | bytes 24580
  3.4 20.3 %copy-start.6 = (bf16[64,64]{1,0:T(8,128)(2,1)S(1)}, bf16[64,64]{1,0:T(8,128)(2,1)}, u32[]{:S(2)}) copy-start(bf16[64,64]{1,0:T(8,128)(2,1)} %constant.32.clone.low_ref) | copy-start | bytes 24580
  25.2 30.0 %all-to-all-start.1 = ((f32[4,16,16,256]{3,2,1,0:T(8,128)}), f32[4,16,16,256]{3,2,1,0:T(8,128)S(1)}, u32[]{:S(2)}, u32[]{:S(2)}) async-start(f32[4,16,16,256]{3,2,1,0:T(8,128)} %y_modes.1), calls=%async_computation.1 | async-start | bytes 2097152 | tf_op jit(solution)/shard_map/all_to_all | solution.py:168
  30.1 0.7 %copy-start.9 = (f32[64]{0:T(128)S(1)}, f32[64]{0:T(128)}, u32[]{:S(2)}) copy-start(f32[64]{0:T(128)} %param.14) | copy-start | bytes 772
  30.8 0.7 %copy-start.10 = (f32[128]{0:T(128)S(1)}, f32[128]{0:T(128)}, u32[]{:S(2)}) copy-start(f32[128]{0:T(128)} %param.13) | copy-start | bytes 1540
  31.6 0.7 %copy-start.8 = (f32[256]{0:T(256)S(1)}, f32[256]{0:T(256)}, u32[]{:S(2)}) copy-start(f32[256]{0:T(256)} %param.15) | copy-start | bytes 3076
  32.3 23.0 %copy-start.1 = (bf16[256,256]{1,0:T(8,128)(2,1)S(1)}, bf16[256,256]{1,0:T(8,128)(2,1)}, u32[]{:S(2)}) copy-start(bf16[256,256]{1,0:T(8,128)(2,1)} %constant.33.clone.refs_1_) | copy-start | bytes 393220
  32.3 23.0 %copy-start.2 = (bf16[256,256]{1,0:T(8,128)(2,1)S(1)}, bf16[256,256]{1,0:T(8,128)(2,1)}, u32[]{:S(2)}) copy-start(bf16[256,256]{1,0:T(8,128)(2,1)} %constant.34.clone.refs_2_) | copy-start | bytes 393220
  32.3 23.0 %copy-start.7 = (f32[4,4]{1,0:T(4,128)S(1)}, f32[4,4]{1,0:T(4,128)}, u32[]{:S(2)}) copy-start(f32[4,4]{1,0:T(4,128)} %refs_4_.1) | copy-start | bytes 196

commit v3 on v2

--- a/solution.py
+++ b/solution.py
@@ -8,7 +8,7 @@
 from jax.experimental.pallas import tpu as pltpu
 from jax.sharding import PartitionSpec as P
 
-SHARES = (1.0,)
+SHARES = (5, 11)
 
 
 def basis_table(count):

time: 58.2 us -> 67.9 us (1.17)
  the two profiles are of different devices: /device:TPU:0 before, /device:TPU:2 now
where the time goes in v3:
time: 67.9 us; the launch traced here: 67.3 us
  waiting for transfers between devices  35.3 us (52%)
  starting transfers between devices  17.7 us (26%)
  Pallas kernels  9.14 us (13%)
  local copies, waits for them, and re-layouts  4.89 us (7%)
    all_to_all x2, waiting for transfers between devices, on_device(): lax.all_to_all(sent, 'deep', split_axis=0, concat_axis=0, tiled=True)  21.3 us
    all_to_all x2, waiting for transfers between devices, on_device(): lax.all_to_all(sent, 'north', split_axis=0, concat_axis=0, tiled=True)  14 us
    all_to_all x2, starting transfers between devices, on_device(): lax.all_to_all(sent, 'north', split_axis=0, concat_axis=0, tiled=True)  9.31 us
    all_to_all x2, starting transfers between devices, on_device(): lax.all_to_all(sent, 'deep', split_axis=0, concat_axis=0, tiled=True)  8.36 us
    unnamed x28, local copies, waits for them, and re-layouts  4.73 us
    pallas_call x2, Pallas kernels, on_device(): pl.pallas_call(functools.partial(z_kernel, first), out_shape=jax.ShapeDty...  3.91 us
    pallas_call x2, Pallas kernels, on_device(): pl.pallas_call(x_kernel, out_shape=jax.ShapeDtypeStruct((north, lanes //...  2.92 us
    pallas_call x2, Pallas kernels, on_device(): pl.pallas_call(y_kernel, out_shape=jax.ShapeDtypeStruct((deep, share, sha...  2.31 us
  transfers between devices with their start and end apart: 4, of which 4 were waited for; matrix products, arithmetic and copies ran while one was open for 1% of the time, Pallas kernels for 8%

profile of v3, /device:TPU:2, one launch (start us, length us, event | category | flops | bytes accessed | tf_op | source)
XLA Modules:
  0.0 67.3 jit_solution(14713281974465776038)
XLA Ops:
  0.0 0.7 %copy-done.8 = bf16[40,128]{1,0:T(8,128)(2,1)S(1)} copy-done((bf16[40,128]{1,0:T(8,128)(2,1)S(1)}, bf16[40,128]{1,0:T(8,128)(2,1)}, u32[]{:S(2)}) %copy-start.8) | copy-done | bytes 10264
  0.7 1.2 %copy-done = f32[4,128,8,64]{1,3,2,0:T(8,128)S(1)} copy-done((f32[4,128,8,64]{1,3,2,0:T(8,128)S(1)}, f32[4,128,8,64]{1,3,2,0:T(8,128)}, u32[]{:S(2)}) %copy-start) | copy-done | bytes 1048600
  1.9 1.4 %x_modes.3 = f32[8,2,40,128]{3,2,1,0:T(8,128)} custom-call(f32[4,8,64,128]{3,2,1,0:T(8,128)S(1)} %bitcast.1, bf16[40,128]{1,0:T(8,128)(2,1)S(1)} %copy-done.9, bf16[40,128]{1,0:T(8,128)(2,1)S(1)} %copy-done.8), custom_call_target="tpu_custom_call" | custom-call | flops 62914560 | bytes 1048576 | tf_op jit(solution)/shard_map/x_modes/pallas_call | solution.py:149
  3.4 4.4 %all-to-all-start.2 = ((f32[8,2,40,128]{3,2,1,0:T(8,128)}), f32[8,2,40,128]{3,2,1,0:T(8,128)S(1)}, u32[]{:S(2)}, u32[]{:S(2)}) async-start(f32[8,2,40,128]{3,2,1,0:T(8,128)} %x_modes.3), calls=%async_computation.2 | async-start | bytes 655360 | tf_op jit(solution)/shard_map/all_to_all | solution.py:158
  7.8 1.5 %x_modes.2 = f32[8,2,88,128]{3,2,1,0:T(8,128)} custom-call(f32[4,8,64,128]{3,2,1,0:T(8,128)S(1)} %bitcast.2, bf16[88,128]{1,0:T(8,128)(2,1)S(1)} %copy-done.7, bf16[88,128]{1,0:T(8,128)(2,1)S(1)} %copy-done.6), custom_call_target="tpu_custom_call" | custom-call | flops 138412032 | bytes 1048576 | tf_op jit(solution)/shard_map/x_modes/pallas_call | solution.py:149
  9.3 4.6 %all-to-all-done.2.values_ref = f32[8,2,40,128]{3,2,1,0:T(8,128)S(1)} async-done(((f32[8,2,40,128]{3,2,1,0:T(8,128)}), f32[8,2,40,128]{3,2,1,0:T(8,128)S(1)}, u32[]{:S(2)}, u32[]{:S(2)}) %all-to-all-start.2) | async-done | bytes 327712 | tf_op jit(solution)/shard_map/all_to_all | solution.py:158
  13.9 4.9 %all-to-all-start = ((f32[8,2,88,128]{3,2,1,0:T(8,128)}), f32[8,2,88,128]{3,2,1,0:T(8,128)S(1)}, u32[]{:S(2)}, u32[]{:S(2)}) async-start(f32[8,2,88,128]{3,2,1,0:T(8,128)} %x_modes.2), calls=%async_computation | async-start | bytes 1441792 | tf_op jit(solution)/shard_map/all_to_all | solution.py:158
  18.8 1.0 %y_modes.3 = f32[4,5,16,256]{3,2,1,0:T(8,128)} custom-call(f32[8,2,40,128]{3,2,1,0:T(8,128)S(1)} %all-to-all-done.2.values_ref, bf16[64,64]{1,0:T(8,128)(2,1)S(1)} %copy-done.5, bf16[64,64]{1,0:T(8,128)(2,1)S(1)} %copy-done.4), custom_call_target="tpu_custom_call" | custom-call | flops 31457280 | bytes 655360 | tf_op jit(solution)/shard_map/y_modes/pallas_call | solution.py:159
  19.8 9.4 %all-to-all-done.values_ref = f32[8,2,88,128]{3,2,1,0:T(8,128)S(1)} async-done(((f32[8,2,88,128]{3,2,1,0:T(8,128)}), f32[8,2,88,128]{3,2,1,0:T(8,128)S(1)}, u32[]{:S(2)}, u32[]{:S(2)}) %all-to-all-start) | async-done | bytes 720928 | tf_op jit(solution)/shard_map/all_to_all | solution.py:158
  29.2 4.9 %all-to-all-start.3 = ((f32[4,5,16,256]{3,2,1,0:T(8,128)}), f32[4,5,16,256]{3,2,1,0:T(8,128)S(1)}, u32[]{:S(2)}, u32[]{:S(2)}) async-start(f32[4,5,16,256]{3,2,1,0:T(8,128)} %y_modes.3), calls=%async_computation.3 | async-start | bytes 655360 | tf_op jit(solution)/shard_map/all_to_all | solution.py:168
  34.1 1.3 %y_modes.2 = f32[4,11,16,256]{3,2,1,0:T(8,128)} custom-call(f32[8,2,88,128]{3,2,1,0:T(8,128)S(1)} %all-to-all-done.values_ref, bf16[64,64]{1,0:T(8,128)(2,1)S(1)} %copy-done.5, bf16[64,64]{1,0:T(8,128)(2,1)S(1)} %copy-done.4), custom_call_target="tpu_custom_call" | custom-call | flops 69206016 | bytes 1441792 | tf_op jit(solution)/shard_map/y_modes/pallas_call | solution.py:159
  35.4 9.2 %all-to-all-done.3.refs_0_ = f32[4,5,16,256]{3,2,1,0:T(8,128)S(1)} async-done(((f32[4,5,16,256]{3,2,1,0:T(8,128)}), f32[4,5,16,256]{3,2,1,0:T(8,128)S(1)}, u32[]{:S(2)}, u32[]{:S(2)}) %all-to-all-start.3) | async-done | bytes 327712 | tf_op jit(solution)/shard_map/all_to_all | solution.py:168
  44.6 3.5 %all-to-all-start.1 = ((f32[4,11,16,256]{3,2,1,0:T(8,128)}), f32[4,11,16,256]{3,2,1,0:T(8,128)S(1)}, u32[]{:S(2)}, u32[]{:S(2)}) async-start(f32[4,11,16,256]{3,2,1,0:T(8,128)} %y_modes.2), calls=%async_computation.1 | async-start | bytes 1441792 | tf_op jit(solution)/shard_map/all_to_all | solution.py:168
  48.1 0.6 copy-done.12
  48.8 0.1 dynamic_slice.7
  48.8 0.6 copy-done.13
  49.4 0.1 dynamic_slice.6
  49.5 0.1 broadcast_add_fusion
  49.6 0.6 copy-done.11
  50.2 0.1 add_divide_fusion
  50.4 0.8 %copy-done.2 = bf16[256,256]{1,0:T(8,128)(2,1)S(1)} copy-done((bf16[256,256]{1,0:T(8,128)(2,1)S(1)}, bf16[256,256]{1,0:T(8,128)(2,1)}, u32[]{:S(2)}) %copy-start.2) | copy-done | bytes 131096
  51.3 1.8 %z_modes.2.refs_5_ = f32[4,16,16,256]{3,2,1,0:T(8,128)} custom-call(f32[4,5,16,256]{3,2,1,0:T(8,128)S(1)} %all-to-all-done.3.refs_0_, bf16[256,256]{1,0:T(8,128)(2,1)S(1)} %copy-done.3, bf16[256,256]{1,0:T(8,128)(2,1)S(1)} %copy-done.2, f32[5,16,256]{2,1,0:T(8,128)S(1)} %slice.9.refs_3_, f32[4,4]{1,0:T(4,128)S(1)} %copy-done.10), custom_call_target="tpu_custom_call" | custom-call | flops 125829120 | bytes 655360 | tf_op jit(solution)/shard_map/z_modes/pallas_call | solution.py:176
  53.1 12.1 %all-to-all-done.1.refs_0_ = f32[4,11,16,256]{3,2,1,0:T(8,128)S(1)} async-done(((f32[4,11,16,256]{3,2,1,0:T(8,128)}), f32[4,11,16,256]{3,2,1,0:T(8,128)S(1)}, u32[]{:S(2)}, u32[]{:S(2)}) %all-to-all-start.1) | async-done | bytes 720928 | tf_op jit(solution)/shard_map/all_to_all | solution.py:168
  65.2 2.1 %z_modes.3 = f32[4,16,16,256]{3,2,1,0:T(8,128)} custom-call(f32[4,11,16,256]{3,2,1,0:T(8,128)S(1)} %all-to-all-done.1.refs_0_, bf16[256,256]{1,0:T(8,128)(2,1)S(1)} %copy-done.3, bf16[256,256]{1,0:T(8,128)(2,1)S(1)} %copy-done.2, f32[11,16,256]{2,1,0:T(8,128)S(1)} %slice.8.refs_3_, f32[4,4]{1,0:T(4,128)S(1)} %copy-done.10, ...), custom_call_target="tpu_custom_call", output_to_operand_aliasing={{}: (5, {})} | custom-call | flops 276824064 | bytes 1441792 | tf_op jit(solution)/shard_map/z_modes/pallas_call | solution.py:176
  (24 shorter events, 0.1 us)
Async XLA Ops:
  0.0 0.7 %copy-start.8 = (bf16[40,128]{1,0:T(8,128)(2,1)S(1)}, bf16[40,128]{1,0:T(8,128)(2,1)}, u32[]{:S(2)}) copy-start(bf16[40,128]{1,0:T(8,128)(2,1)} %constant.40.clone.low_ref) | copy-start | bytes 30724
  0.0 0.7 %copy-start.9 = (bf16[40,128]{1,0:T(8,128)(2,1)S(1)}, bf16[40,128]{1,0:T(8,128)(2,1)}, u32[]{:S(2)}) copy-start(bf16[40,128]{1,0:T(8,128)(2,1)} %constant.39.clone.high_ref) | copy-start | bytes 30724
  0.7 1.2 %copy-start = (f32[4,128,8,64]{1,3,2,0:T(8,128)S(1)}, f32[4,128,8,64]{1,3,2,0:T(8,128)}, u32[]{:S(2)}) copy-start(f32[4,128,8,64]{1,3,2,0:T(8,128)} %param.13) | copy-start | bytes 3145732
  1.9 5.8 %copy-start.1 = (f32[4,128,8,64]{1,3,2,0:T(8,128)S(1)}, f32[4,128,8,64]{1,3,2,0:T(8,128)}, u32[]{:S(2)}) copy-start(f32[4,128,8,64]{1,3,2,0:T(8,128)} %param.13) | copy-start | bytes 3145732
  3.4 4.4 %copy-start.6 = (bf16[88,128]{1,0:T(8,128)(2,1)S(1)}, bf16[88,128]{1,0:T(8,128)(2,1)}, u32[]{:S(2)}) copy-start(bf16[88,128]{1,0:T(8,128)(2,1)} %constant.42.clone.low_ref) | copy-start | bytes 67588
  3.4 4.4 %copy-start.7 = (bf16[88,128]{1,0:T(8,128)(2,1)S(1)}, bf16[88,128]{1,0:T(8,128)(2,1)}, u32[]{:S(2)}) copy-start(bf16[88,128]{1,0:T(8,128)(2,1)} %constant.41.clone.high_ref) | copy-start | bytes 67588
  3.4 10.5 %all-to-all-start.2 = ((f32[8,2,40,128]{3,2,1,0:T(8,128)}), f32[8,2,40,128]{3,2,1,0:T(8,128)S(1)}, u32[]{:S(2)}, u32[]{:S(2)}) async-start(f32[8,2,40,128]{3,2,1,0:T(8,128)} %x_modes.3), calls=%async_computation.2 | async-start | bytes 655360 | tf_op jit(solution)/shard_map/all_to_all | solution.py:158
  9.3 9.5 %copy-start.4 = (bf16[64,64]{1,0:T(8,128)(2,1)S(1)}, bf16[64,64]{1,0:T(8,128)(2,1)}, u32[]{:S(2)}) copy-start(bf16[64,64]{1,0:T(8,128)(2,1)} %constant.36.clone.low_ref) | copy-start | bytes 24580
  9.3 9.5 %copy-start.5 = (bf16[64,64]{1,0:T(8,128)(2,1)S(1)}, bf16[64,64]{1,0:T(8,128)(2,1)}, u32[]{:S(2)}) copy-start(bf16[64,64]{1,0:T(8,128)(2,1)} %constant.35.clone.high_ref) | copy-start | bytes 24580
  13.9 15.3 %all-to-all-start = ((f32[8,2,88,128]{3,2,1,0:T(8,128)}), f32[8,2,88,128]{3,2,1,0:T(8,128)S(1)}, u32[]{:S(2)}, u32[]{:S(2)}) async-start(f32[8,2,88,128]{3,2,1,0:T(8,128)} %x_modes.2), calls=%async_computation | async-start | bytes 1441792 | tf_op jit(solution)/shard_map/all_to_all | solution.py:158
  29.2 15.4 %all-to-all-start.3 = ((f32[4,5,16,256]{3,2,1,0:T(8,128)}), f32[4,5,16,256]{3,2,1,0:T(8,128)S(1)}, u32[]{:S(2)}, u32[]{:S(2)}) async-start(f32[4,5,16,256]{3,2,1,0:T(8,128)} %y_modes.3), calls=%async_computation.3 | async-start | bytes 655360 | tf_op jit(solution)/shard_map/all_to_all | solution.py:168
  44.6 20.6 %all-to-all-start.1 = ((f32[4,11,16,256]{3,2,1,0:T(8,128)}), f32[4,11,16,256]{3,2,1,0:T(8,128)S(1)}, u32[]{:S(2)}, u32[]{:S(2)}) async-start(f32[4,11,16,256]{3,2,1,0:T(8,128)} %y_modes.2), calls=%async_computation.1 | async-start | bytes 1441792 | tf_op jit(solution)/shard_map/all_to_all | solution.py:168
  48.1 0.7 copy-start.12
  48.8 0.7 copy-start.13
  49.5 0.7 %copy-start.11 = (f32[256]{0:T(256)S(1)}, f32[256]{0:T(256)}, u32[]{:S(2)}) copy-start(f32[256]{0:T(256)} %param.17) | copy-start | bytes 3076
  50.3 0.9 %copy-start.2 = (bf16[256,256]{1,0:T(8,128)(2,1)S(1)}, bf16[256,256]{1,0:T(8,128)(2,1)}, u32[]{:S(2)}) copy-start(bf16[256,256]{1,0:T(8,128)(2,1)} %constant.38.clone.refs_2_) | copy-start | bytes 393220
  50.3 1.0 %copy-start.3 = (bf16[256,256]{1,0:T(8,128)(2,1)S(1)}, bf16[256,256]{1,0:T(8,128)(2,1)}, u32[]{:S(2)}) copy-start(bf16[256,256]{1,0:T(8,128)(2,1)} %constant.37.clone.refs_1_) | copy-start | bytes 393220
  50.3 1.0 %copy-start.10 = (f32[4,4]{1,0:T(4,128)S(1)}, f32[4,4]{1,0:T(4,128)}, u32[]{:S(2)}) copy-start(f32[4,4]{1,0:T(4,128)} %refs_4_.3) | copy-start | bytes 196
